TPU v7x, 16 devices: a 4x2x1 block of a 4x4x8 slice. The times are simulated.
16 devices in a mesh: data: 2 (over y, z), seq: 8 (over x, core).
Axes of the slice: x: 4, y: 2, z: 1, core: 2. Of those that a mesh axis runs over, the one named last changes fastest.
The devices are a block of a 4x4x8 slice.
Arguments:
- x_tokens: bfloat16 [128, 512, 768], P('data', 'seq'), parts along dimension 0
- lengths: int32 [128], P('data'), parts along dimension 0
- phi_slots: bfloat16 [768, 128], replicated
- scale_g: float32 [], replicated
- w_in: bfloat16 [128, 768, 3072], P('seq')
- w_out: bfloat16 [128, 3072, 768], P('seq')
- ws_in: bfloat16 [768, 3072], replicated
- ws_out: bfloat16 [3072, 768], replicated
Outputs:
- output: bfloat16 [128, 512, 768], P('data', 'seq'), parts along dimension 0
There are 2 independent parts. A program takes and returns all parts, laid end to end along the dimension named above; an argument that names none is the same for every part.
All inputs are finite; a program needn't handle non-finite values.
Results may differ from a plain program's by a relative error of at most 0.0133919.
Values are sent between devices in bfloat16 or wider.
A program may use at most 768 MiB of HBM per device.

v0:
```python
import functools

import jax
import jax.numpy as jnp
from jax import lax
from jax.experimental import pallas as pl
from jax.experimental.pallas import tpu as pltpu
from jax.sharding import PartitionSpec as P

NORM_EPS = 1e-6
NEG_BIG = -1e30
F32 = jnp.float32
BF16 = jnp.bfloat16
MESH = pl.DeviceIdType.MESH
LANES = 128
NGRP = 2
NCHUNK = 4
ER = 8
VMEM_BYTES = 67043328

D2D, TUP, TDN, RUP, RDN, SUP, SDN = range(7)
OUP, ODN, OPA, FUP, FDN, PUP, PDN, PLO, PHI = range(9)


def unit_rows(values, axis_id):
    wide_vals = values.astype(F32)
    return wide_vals / jnp.sqrt(jnp.sum(wide_vals * wide_vals, axis=axis_id, keepdims=True) + NORM_EPS)


def dot(a, b):
    return jnp.dot(a, b, preferred_element_type=F32)


def gelu(v):
    return jax.nn.gelu(v, approximate=True)


def front_kernel(tok, len_ref, x_ref, phi_ref, xn_ref, lm_ref, mix_ref, pm_ref):
    blk = pl.program_id(0)
    first = lax.axis_index('seq') * tok
    pairs = pm_ref.shape[0]
    rows, cols = 2 * tok, phi_ref.shape[1]

    def body(p, _):
        sl = pl.ds(pl.multiple_of(p * rows, rows), rows)
        x = x_ref[sl, :].astype(F32)
        inv = lax.rsqrt(jnp.sum(x * x, axis=1, keepdims=True) + NORM_EPS)
        xn = (x * inv).astype(BF16)
        xn_ref[sl, :] = xn
        logits = dot(xn, phi_ref[...])
        seq0 = 2 * (blk * pairs + p)
        ri = lax.broadcasted_iota(jnp.int32, (rows, cols), 0)
        ci = lax.broadcasted_iota(jnp.int32, (rows, cols), 1)
        odd = ri >= tok
        same = jnp.where(odd, 1, 0) == ((ci >> 3) & 1)
        lim = jnp.where(odd, len_ref[seq0 + 1], len_ref[seq0])
        valid = (first + (ri & (tok - 1))) < lim
        own = jnp.where(same, logits, NEG_BIG)
        top = jnp.max(own, axis=1, keepdims=True)
        ex = jnp.exp(own - top)
        mix_ref[sl, :] = (ex / jnp.sum(ex, axis=1, keepdims=True)).astype(BF16)
        lm = jnp.where(valid, own, NEG_BIG)
        lm_ref[sl, :] = lm
        pm_ref[pl.ds(p, 1), :] = jnp.max(lm, axis=0, keepdims=True)
        return 0

    lax.fori_loop(0, pairs, body, 0)


def mega_kernel(n, x_hbm, lm_hbm, xn_hbm, pm, wsi_hbm, wso_hbm, w1_hbm, w2_hbm,
                g_hbm, y2_hbm,
                part, dbuf, tbuf, rbuf, wsi, wso, w1b, w2b, xb, lb, xnb, y2b, sbuf, yb,
                mxb, mx, zs, zt, zb, zo,
                rs_s, rs_r, ag_s, ag_r, mx_s, mx_r, z_s, z_r, xl_sem, ws_sem, w_sem, xn_sem, y2_sem, loc_sem):
    me = lax.axis_index('seq')
    chip, core = me // 2, me % 2
    chips = n // 2
    mate = chip * 2 + (1 - core)
    cup, cdn, cop = (chip + 1) % chips, (chip + chips - 1) % chips, (chip + 2) % chips
    up, dn = cup * 2 + core, cdn * 2 + core
    npair = pm.shape[0]
    pc = npair // NCHUNK
    ph = pc // 2
    rows = lb.shape[1] // pc
    dwidth = xb.shape[2]
    ntile = dwidth // LANES
    dtok = xnb.shape[1]
    dtiles = y2_hbm.shape[0] // dtok

    def rdma(src, dst, ss, rs, dev):
        return pltpu.make_async_remote_copy(src_ref=src, dst_ref=dst, send_sem=ss, recv_sem=rs,
                                            device_id={'seq': dev}, device_id_type=MESH)

    def xl_load(c, slot):
        ps = pl.ds(pl.multiple_of(c * pc * rows, pc * rows), pc * rows)
        return (pltpu.make_async_copy(x_hbm.at[ps, :], xb.at[slot], xl_sem.at[0, slot]),
                pltpu.make_async_copy(lm_hbm.at[ps, :], lb.at[slot], xl_sem.at[1, slot]))

    def w_load(e, slot):
        return (pltpu.make_async_copy(w1_hbm.at[e], w1b.at[slot], w_sem.at[0, slot]),
                pltpu.make_async_copy(w2_hbm.at[e], w2b.at[slot], w_sem.at[1, slot]))

    def ws_load():
        return (pltpu.make_async_copy(wsi_hbm, wsi, ws_sem.at[0]),
                pltpu.make_async_copy(wso_hbm, wso, ws_sem.at[1]))

    def xn_load(i, slot):
        ps = pl.ds(pl.multiple_of(i * dtok, dtok), dtok)
        return pltpu.make_async_copy(xn_hbm.at[ps, :], xnb.at[slot], xn_sem.at[slot])

    def y2_store(i, slot):
        ps = pl.ds(pl.multiple_of(i * dtok, dtok), dtok)
        return pltpu.make_async_copy(y2b.at[slot], y2_hbm.at[ps, :], y2_sem.at[slot])

    def start(copies):
        for cp in copies:
            cp.start()

    def all_of(c):
        return pl.ds(c * pc, pc)

    def lo_of(c):
        return pl.ds(c * pc, ph)

    def hi_of(c):
        return pl.ds(c * pc + ph, ph)

    def rs(kind, g, c):
        ss, rr = rs_s.at[kind, g, c], rs_r.at[kind, g, c]
        mine = part.at[g, core]
        if kind == D2D:
            return rdma(part.at[g, 1 - core, :, all_of(c)], dbuf.at[g, :, all_of(c)], ss, rr, mate)
        if kind == TUP:
            return rdma(mine.at[cop, lo_of(c)], tbuf.at[0, g, pl.ds(c * ph, ph)], ss, rr, up)
        if kind == TDN:
            return rdma(mine.at[cop, hi_of(c)], tbuf.at[1, g, pl.ds(c * ph, ph)], ss, rr, dn)
        if kind == RUP:
            return rdma(mine.at[cup, hi_of(c)], rbuf.at[0, g, hi_of(c)], ss, rr, up)
        if kind == RDN:
            return rdma(mine.at[cdn, lo_of(c)], rbuf.at[1, g, lo_of(c)], ss, rr, dn)
        if kind == SUP:
            return rdma(mine.at[cup, lo_of(c)], rbuf.at[0, g, lo_of(c)], ss, rr, up)
        return rdma(mine.at[cdn, hi_of(c)], rbuf.at[1, g, hi_of(c)], ss, rr, dn)

    def stage1(g, c):
        rs(D2D, g, c).wait_recv()

        def body(i, _):
            q = c * pc + i
            a = part[g, core, :, q].astype(F32) + dbuf[g, :, q].astype(F32)
            part[g, core, :, q] = a.astype(BF16)
            return 0

        lax.fori_loop(0, pc, body, 0)
        for kind in (TUP, TDN, RUP, RDN):
            rs(kind, g, c).start()

    def stage2(g, c):
        for kind, nxt, dst, off, d in ((TUP, SUP, cup, 0, 0), (TDN, SDN, cdn, ph, 1)):
            rs(kind, g, c).wait_recv()

            def body(i, _):
                q = c * pc + off + i
                a = part[g, core, dst, q].astype(F32) + tbuf[d, g, c * ph + i].astype(F32)
                part[g, core, dst, q] = a.astype(BF16)
                return 0

            lax.fori_loop(0, ph, body, 0)
            rs(nxt, g, c).start()

    def stage3(g, c):
        for kind in (RUP, RDN, SUP, SDN):
            rs(kind, g, c).wait_recv()
        zg = zo[...]
        lane = lax.broadcasted_iota(jnp.int32, zg.shape, 1)

        def body(i, _):
            q = c * pc + i
            z = jnp.sum(jnp.where(lane == g * npair + q, zg, 0.0), axis=1, keepdims=True)
            a = part[g, core, chip, q].astype(F32) + rbuf[0, g, q].astype(F32) + rbuf[1, g, q].astype(F32)
            a = a / z
            for j in range(ntile):
                sbuf[j, pl.ds(pl.multiple_of(q * 16, 16), 16), :] = a[:, j * LANES:(j + 1) * LANES]
            return 0

        lax.fori_loop(0, pc, body, 0)

    def ag(kind, g, c):
        ss, rr = ag_s.at[kind, g, c], ag_r.at[kind, g, c]
        if kind in (OUP, ODN, OPA):
            return rdma(yb.at[g, all_of(c)], g_hbm.at[g, core, chip, all_of(c)], ss, rr,
                        {OUP: up, ODN: dn, OPA: mate}[kind])
        origin, part_of, dev = {FUP: (cdn, lo_of, up), FDN: (cup, hi_of, dn),
                                PUP: (cdn, all_of, mate), PDN: (cup, all_of, mate),
                                PLO: (cop, lo_of, mate), PHI: (cop, hi_of, mate)}[kind]
        ref = g_hbm.at[g, core, origin, part_of(c)]
        return rdma(ref, ref, ss, rr, dev)

    def own_copy(g, c):
        return pltpu.make_async_copy(yb.at[g, all_of(c)], g_hbm.at[g, core, chip, all_of(c)], loc_sem.at[g, c])

    def send_own(g):
        def body(q, _):
            for j in range(ntile):
                yb[g, q, :, j * LANES:(j + 1) * LANES] = sbuf[j, pl.ds(pl.multiple_of(q * 16, 16), 16), :].astype(BF16)
            return 0

        for c in range(NCHUNK):
            lax.fori_loop(c * pc, (c + 1) * pc, body, 0)
            for kind in (OUP, ODN, OPA):
                ag(kind, g, c).start()
            own_copy(g, c).start()

    def relay1(g, c):
        ag(OUP, g, c).wait_recv()
        ag(FUP, g, c).start()
        ag(PUP, g, c).start()
        ag(ODN, g, c).wait_recv()
        ag(FDN, g, c).start()
        ag(PDN, g, c).start()

    def relay2(g, c):
        ag(FUP, g, c).wait_recv()
        ag(PLO, g, c).start()
        ag(FDN, g, c).wait_recv()
        ag(PHI, g, c).start()

    def dense_tile(i):
        slot = i % 2
        xn_load(i, slot).wait()
        xt = xnb[slot]
        hidden = wsi.shape[1]
        step = min(hidden, 768)
        acc = None
        for f in range(0, hidden, step):
            h = gelu(dot(xt, wsi[:, f:f + step])).astype(BF16)
            o = dot(h, wso[f:f + step, :])
            acc = o if acc is None else acc + o

        @pl.when(i >= 2)
        def _():
            y2_store(i - 2, slot).wait()

        y2b[slot] = acc
        y2_store(i, slot).start()

        @pl.when(i + 2 < dtiles)
        def _():
            xn_load(i + 2, slot).start()

    def expert(g, e, total):
        idx = g * ER + e
        slot = idx % 2
        xin = jnp.concatenate([sbuf[j, pl.ds(e, 2 * npair, stride=ER), :] for j in range(ntile)], axis=1).astype(BF16)
        l1, l2 = w_load(idx, slot)
        l1.wait()
        l2.wait()
        hidden = w1b.shape[2]
        step = min(hidden, 768)
        acc = None
        for f in range(0, hidden, step):
            h = gelu(dot(xin, w1b[slot, :, f:f + step])).astype(BF16)
            o = dot(h, w2b[slot, f:f + step, :])
            acc = o if acc is None else acc + o
        for j in range(ntile):
            sbuf[j, pl.ds(e, 2 * npair, stride=ER), :] = acc[:, j * LANES:(j + 1) * LANES]

        @pl.when(idx + 2 < total)
        def _():
            start(w_load(idx + 2, slot))

    start(xl_load(0, 0))
    start(xl_load(1, 1))
    barrier = pltpu.get_barrier_semaphore()
    for k in range(1, n):
        pl.semaphore_signal(barrier, inc=1, device_id={'seq': lax.rem(me + k, n)}, device_id_type=MESH)
    zs[...] = jnp.zeros_like(zs)
    pl.semaphore_wait(barrier, n - 1)

    def mx_msg(k):
        return rdma(pm, mxb.at[me], mx_s.at[k - 1], mx_r.at[k - 1], lax.rem(me + k, n))

    for k in range(1, n):
        mx_msg(k).start()
    start(ws_load())
    xn_load(0, 0).start()
    xn_load(1, 1).start()
    for k in range(1, n):
        mx_msg(k).wait_recv()
    top = pm[...]
    for k in range(1, n):
        top = jnp.maximum(top, mxb[lax.rem(me + n - k, n)])
    mx[...] = top

    half = lb.shape[2] // 2

    def num_chunk(c, _):
        slot = c % 2
        for cp in xl_load(c, slot):
            cp.wait()

        def body(i, _):
            q = c * pc + i
            sl = pl.ds(pl.multiple_of(i * rows, rows), rows)
            e = jnp.exp(lb[slot, sl, :] - mx[pl.ds(q, 1), :])
            z = jnp.sum(e, axis=0, keepdims=True)
            zs[pl.ds(q, 1), :] = z[:, :half]
            zs[pl.ds(npair + q, 1), :] = z[:, half:]
            num = lax.dot_general(e.astype(BF16), xb[slot, sl, :], (((0,), (0,)), ((), ())),
                                  preferred_element_type=F32)
            part[:, :, :, q] = num.astype(BF16).reshape(NGRP, 2, chips, 16, dwidth)
            return 0

        lax.fori_loop(0, pc, body, 0)
        for g in range(NGRP):
            rs(D2D, g, c).start()

        @pl.when(c + 2 < NCHUNK)
        def _():
            start(xl_load(c + 2, slot))

        @pl.when(c >= 1)
        def _():
            stage1(0, c - 1)

        return 0

    lax.fori_loop(0, NCHUNK, num_chunk, 0)
    start(w_load(0, 0))
    start(w_load(1, 1))
    stage1(0, NCHUNK - 1)

    zt[...] = zs[...].T.reshape(zt.shape)

    def z_msg(k):
        dev = lax.rem(me + k, n)
        return rdma(zt.at[dev % 2, dev // 2], zb.at[me], z_s.at[k - 1], z_r.at[k - 1], dev)

    for k in range(1, n):
        z_msg(k).start()
    for cp in ws_load():
        cp.wait()

    def dense_a(i, _):
        dense_tile(i)

        @pl.when(i < NCHUNK)
        def _():
            stage2(0, i)

        @pl.when((i >= NCHUNK) & (i < 2 * NCHUNK))
        def _():
            stage1(1, i - NCHUNK)

        return 0

    lax.fori_loop(0, dtiles // 2, dense_a, 0)

    for k in range(1, n):
        z_msg(k).wait_recv()
    ztot = zt[core, chip]
    for k in range(1, n):
        ztot = ztot + zb[lax.rem(me + n - k, n)]
    zo[...] = ztot

    def run3(g):
        def body(c, _):
            stage3(g, c)
            return 0

        lax.fori_loop(0, NCHUNK, body, 0)

    run3(0)

    total = NGRP * ER

    def experts_a(e, _):
        expert(0, e, total)

        @pl.when(e < NCHUNK)
        def _():
            stage2(1, e)

        return 0

    lax.fori_loop(0, ER, experts_a, 0)
    send_own(0)
    run3(1)

    def experts_b(e, _):
        expert(1, e, total)

        @pl.when(e < NCHUNK)
        def _():
            relay1(0, e)

        @pl.when(e >= NCHUNK)
        def _():
            relay2(0, e - NCHUNK)

        return 0

    lax.fori_loop(0, ER, experts_b, 0)
    send_own(1)

    def dense_b(i, _):
        dense_tile(dtiles // 2 + i)

        @pl.when(i < NCHUNK)
        def _():
            relay1(1, i)

        @pl.when((i >= NCHUNK) & (i < 2 * NCHUNK))
        def _():
            relay2(1, i - NCHUNK)

        return 0

    lax.fori_loop(0, dtiles // 2, dense_b, 0)

    y2_store(dtiles - 2, 0).wait()
    y2_store(dtiles - 1, 1).wait()
    for k in range(1, n):
        mx_msg(k).wait_send()
        z_msg(k).wait_send()

    def drain(c, _):
        for g in range(NGRP):
            for kind in range(7):
                rs(kind, g, c).wait_send()
            for kind in range(9):
                ag(kind, g, c).wait_send()
            own_copy(g, c).wait()
            for kind in (OPA, PUP, PDN, PLO, PHI):
                ag(kind, g, c).wait_recv()
        return 0

    lax.fori_loop(0, NCHUNK, drain, 0)


def combine_kernel(g_ref, mix_ref, y2_ref, y_ref):
    pairs = g_ref.shape[3]
    cols = mix_ref.shape[1]
    rows = mix_ref.shape[0] // pairs

    def body(p, _):
        sl = pl.ds(pl.multiple_of(p * rows, rows), rows)
        rhs = g_ref[:, :, :, p].reshape(cols, g_ref.shape[5])
        y_ref[sl, :] = (dot(mix_ref[sl, :], rhs) + y2_ref[sl, :]).astype(BF16)
        return 0

    lax.fori_loop(0, pairs, body, 0)


def solution(mesh):
    n = mesh.shape['seq']
    chips = n // 2
    tok_spec = P('data', 'seq', None)
    expert_spec = P('seq', None, None)

    def per_device(x_blk, len_blk, phi_slots, scale_g, w_in_blk, w_out_blk, ws_in, ws_out):
        batch, tok, width = x_blk.shape
        slots = phi_slots.shape[1]
        hidden = ws_in.shape[1]
        cols = 2 * slots
        npair = batch // 2
        ntok = batch * tok
        x2 = x_blk.reshape(ntok, width)
        phi_norm = (scale_g * unit_rows(phi_slots, 0)).astype(BF16)
        phi_cols = phi_norm.reshape(width, chips, 2, NGRP, ER).transpose(0, 3, 2, 1, 4)
        phi_cols = jnp.broadcast_to(phi_cols[:, :, :, :, None, :], (width, NGRP, 2, chips, 2, ER)).reshape(width, cols)

        fb = 4
        ft = ntok // fb
        xn, lm, mix, pm = pl.pallas_call(
            functools.partial(front_kernel, tok),
            grid_spec=pltpu.PrefetchScalarGridSpec(
                num_scalar_prefetch=1,
                grid=(fb,),
                in_specs=[pl.BlockSpec((ft, width), lambda i, l: (i, 0)),
                          pl.BlockSpec((width, cols), lambda i, l: (0, 0))],
                out_specs=[pl.BlockSpec((ft, width), lambda i, l: (i, 0)),
                           pl.BlockSpec((ft, cols), lambda i, l: (i, 0)),
                           pl.BlockSpec((ft, cols), lambda i, l: (i, 0)),
                           pl.BlockSpec((npair // fb, cols), lambda i, l: (i, 0))]),
            out_shape=[jax.ShapeDtypeStruct((ntok, width), BF16),
                       jax.ShapeDtypeStruct((ntok, cols), F32),
                       jax.ShapeDtypeStruct((ntok, cols), BF16),
                       jax.ShapeDtypeStruct((npair, cols), F32)],
            name='front',
        )(len_blk, x2, phi_cols)

        pc = npair // NCHUNK
        rows = 2 * tok
        dtok = ntok // 16
        any_spec = pl.BlockSpec(memory_space=pl.ANY)
        sem = pltpu.SemaphoreType.DMA
        slot_out, y2 = pl.pallas_call(
            functools.partial(mega_kernel, n),
            in_specs=[any_spec, any_spec, any_spec, pl.BlockSpec(memory_space=pltpu.VMEM),
                      any_spec, any_spec, any_spec, any_spec],
            out_specs=[any_spec, any_spec],
            out_shape=[jax.ShapeDtypeStruct((NGRP, 2, chips, npair, 16, width), BF16),
                       jax.ShapeDtypeStruct((ntok, width), F32)],
            scratch_shapes=[
                pltpu.VMEM((NGRP, 2, chips, npair, 16, width), BF16),
                pltpu.VMEM((NGRP, chips, npair, 16, width), BF16),
                pltpu.VMEM((2, NGRP, npair // 2, 16, width), BF16),
                pltpu.VMEM((2, NGRP, npair, 16, width), BF16),
                pltpu.VMEM((width, hidden), BF16),
                pltpu.VMEM((hidden, width), BF16),
                pltpu.VMEM((2, width, hidden), BF16),
                pltpu.VMEM((2, hidden, width), BF16),
                pltpu.VMEM((2, pc * rows, width), BF16),
                pltpu.VMEM((2, pc * rows, cols), F32),
                pltpu.VMEM((2, dtok, width), BF16),
                pltpu.VMEM((2, dtok, width), F32),
                pltpu.VMEM((width // LANES, npair * 16, LANES), F32),
                pltpu.VMEM((NGRP, npair, 16, width), BF16),
                pltpu.VMEM((n, npair, cols), F32),
                pltpu.VMEM((npair, cols), F32),
                pltpu.VMEM((LANES, cols // 2), F32),
                pltpu.VMEM((2, chips, 16, LANES), F32),
                pltpu.VMEM((n, 16, LANES), F32),
                pltpu.VMEM((16, LANES), F32),
                sem((7, NGRP, NCHUNK)), sem((7, NGRP, NCHUNK)),
                sem((9, NGRP, NCHUNK)), sem((9, NGRP, NCHUNK)),
                sem((n - 1,)), sem((n - 1,)), sem((n - 1,)), sem((n - 1,)),
                sem((2, 2)), sem((2,)), sem((2, 2)), sem((2,)), sem((2,)), sem((NGRP, NCHUNK)),
            ],
            compiler_params=pltpu.CompilerParams(collective_id=0, has_side_effects=True,
                                                 vmem_limit_bytes=VMEM_BYTES),
            name='mega',
        )(x2, lm, xn, pm, ws_in, ws_out, w_in_blk, w_out_blk)

        cb = 8
        ct = ntok // cb
        y = pl.pallas_call(
            combine_kernel,
            grid=(cb,),
            in_specs=[pl.BlockSpec((NGRP, 2, chips, npair // cb, 16, width), lambda i: (0, 0, 0, i, 0, 0)),
                      pl.BlockSpec((ct, cols), lambda i: (i, 0)),
                      pl.BlockSpec((ct, width), lambda i: (i, 0))],
            out_specs=pl.BlockSpec((ct, width), lambda i: (i, 0)),
            out_shape=jax.ShapeDtypeStruct((ntok, width), BF16),
            name='combine',
        )(slot_out, mix, y2)
        return y.reshape(batch, tok, width)

    return jax.shard_map(per_device, mesh=mesh, in_specs=(tok_spec, P('data'), P(), P(), expert_spec, expert_spec, P(), P()), out_specs=tok_spec, check_vma=False)
```

profile of v0, /device:TPU:113, one launch (start us, length us, event | category | flops | bytes accessed | tf_op | source)
XLA Modules:
  0.0 176.3 jit_solution(8479056455203647834)
XLA Ops:
  0.7 1.1 copy.10
  1.7 0.1 fusion
  1.8 0.1 fusion.2
  2.0 0.9 copy.12.phi_ref
  3.0 18.5 %front.1 = (bf16[4096,768]{1,0:T(8,128)(2,1)}, f32[4096,256]{1,0:T(8,128)}, bf16[4096,256]{1,0:T(8,128)(2,1)}, f32[32,256]{1,0:T(8,128)}) custom-call(s32[64]{0:T(128)} %len_ref.1, bf16[4096,768]{1,0:T(8,128)(2,1)} %bitcast.6, bf16[768,256]{1,0:T(8,128)(2,1)} %copy.12.phi_ref), custom_call_target="tpu_custom_call" | custom-call | tf_op jit(solution)/shard_map/front/pallas_call | solution.py:475
  21.4 139.6 %mega.1 = (bf16[2,2,4,32,16,768]{5,4,3,2,1,0:T(8,128)(2,1)}, f32[4096,768]{1,0:T(8,128)}) custom-call(bf16[4096,768]{1,0:T(8,128)(2,1)} %bitcast.7, f32[4096,256]{1,0:T(8,128)} %get-tuple-element.11.lm_hbm, bf16[4096,768]{1,0:T(8,128)(2,1)} %get-tuple-element.12.xn_hbm, f32[32,256]{1,0:T(8,128)} %get-tuple-element.13.pm, bf16[768,3072]{1,0:T(8,128)(2,1)} %wsi_hbm.1, ...), custom_call_target="tpu_custom_call" | custom-call | tf_op jit(solution)/shard_map/mega/pallas_call | solution.py:498
  161.0 15.2 %combine.1 = bf16[4096,768]{1,0:T(8,128)(2,1)} custom-call(bf16[2,2,4,32,16,768]{5,4,3,2,1,0:T(8,128)(2,1)} %get-tuple-element.14.g_ref, bf16[4096,256]{1,0:T(8,128)(2,1)} %get-tuple-element.15.mix_ref, f32[4096,768]{1,0:T(8,128)} %get-tuple-element.16.y2_ref), custom_call_target="tpu_custom_call" | custom-call | tf_op jit(solution)/shard_map/combine/pallas_call | solution.py:538
  (3 shorter events, 0.1 us)
where the time goes:
time: 176 us
  Pallas kernels  173 us (98%)
  local copies, waits for them, and re-layouts  2.01 us (1%)
    pallas_call x1, Pallas kernels, per_device(): pl.pallas_call(functools.partial(mega_kernel, n), in_specs=[any_spec, any...  140 us
    pallas_call x1, Pallas kernels, per_device(): pl.pallas_call(functools.partial(front_kernel, tok), grid_spec=pltpu.Pref...  18.5 us
    pallas_call x1, Pallas kernels, per_device(): pl.pallas_call(combine_kernel, grid=(cb,), in_specs=[pl.BlockSpec((NGRP,...  15.2 us

commit v1 on v0

v1 whole, which is shorter than its diff:
```python
import functools

import jax
import jax.numpy as jnp
from jax import lax
from jax.experimental import pallas as pl
from jax.experimental.pallas import tpu as pltpu
from jax.sharding import PartitionSpec as P

NORM_EPS = 1e-6
NEG_BIG = -1e30
F32 = jnp.float32
BF16 = jnp.bfloat16
MESH = pl.DeviceIdType.MESH
LANES = 128
NGRP = 2
NCHUNK = 4
ER = 8
VMEM_BYTES = 67043328
UNROLL = 4
DTOK = 256
DENSE_A = 6
DENSE_E = ()

D2D, TUP, TDN, RUP, RDN, SUP, SDN = range(7)
OUP, ODN, OPA, FUP, FDN, PUP, PDN, PLO, PHI = range(9)


def unit_rows(values, axis_id):
    wide_vals = values.astype(F32)
    return wide_vals / jnp.sqrt(jnp.sum(wide_vals * wide_vals, axis=axis_id, keepdims=True) + NORM_EPS)


def dot(a, b):
    return jnp.dot(a, b, preferred_element_type=F32)


def gelu(v):
    return jax.nn.gelu(v, approximate=True)


def mega_kernel(n, tok, len_ref, phi, x_hbm, wsi_hbm, wso_hbm, w1_hbm, w2_hbm,
                y_hbm, y2_hbm, xn_hbm,
                part, dbuf, tbuf, rbuf, wsi, wso, w1b, w2b, lb, mixb, xnb, y2b, y2c, yt, sbuf,
                pm, mxb, mx, zs, zt, zb, zo,
                rs_s, rs_r, ag_s, ag_r, mx_s, mx_r, z_s, z_r, x_sem, xs_sem, ws_sem, w_sem, xn_sem, y2_sem,
                yc_sem, yt_sem, free_sem):
    me = lax.axis_index('seq')
    chip, core = me // 2, me % 2
    chips = n // 2
    mate = chip * 2 + (1 - core)
    cup, cdn, cop = (chip + 1) % chips, (chip + chips - 1) % chips, (chip + 2) % chips
    up, dn = cup * 2 + core, cdn * 2 + core
    npair, cols = pm.shape
    pc = npair // NCHUNK
    ph = pc // 2
    rows = 2 * tok
    crows = pc * rows
    dwidth = phi.shape[0]
    ntile = dwidth // LANES
    dtiles = y2_hbm.shape[0] // DTOK
    per = w2b.shape[1] // crows

    def rdma(src, dst, ss, rs, dev):
        return pltpu.make_async_remote_copy(src_ref=src, dst_ref=dst, send_sem=ss, recv_sem=rs,
                                            device_id={'seq': dev}, device_id_type=MESH)

    def w2_rows(block, off, size):
        return block // per, pl.ds(pl.multiple_of((block % per) * crows + off, rows), size)

    def tok_rows(c):
        return pl.ds(pl.multiple_of(c * crows, crows), crows)

    def x_load(c):
        b, sl = w2_rows(c, 0, crows)
        return pltpu.make_async_copy(x_hbm.at[tok_rows(c), :], w2b.at[b, sl, :], x_sem.at[c])

    def xn_store(c):
        b, sl = w2_rows(NCHUNK + c % 2, 0, crows)
        return pltpu.make_async_copy(w2b.at[b, sl, :], xn_hbm.at[tok_rows(c), :], xs_sem.at[c % 2])

    def w_load(e, slot):
        return (pltpu.make_async_copy(w1_hbm.at[e], w1b.at[slot], w_sem.at[0, slot]),
                pltpu.make_async_copy(w2_hbm.at[e], w2b.at[slot], w_sem.at[1, slot]))

    def ws_load():
        return (pltpu.make_async_copy(wsi_hbm, wsi, ws_sem.at[0]),
                pltpu.make_async_copy(wso_hbm, wso, ws_sem.at[1]))

    def tile_rows(i):
        return pl.ds(pl.multiple_of(i * DTOK, DTOK), DTOK)

    def xn_load(i, slot):
        return pltpu.make_async_copy(xn_hbm.at[tile_rows(i), :], xnb.at[slot], xn_sem.at[slot])

    def y2_store(i, slot):
        return pltpu.make_async_copy(y2b.at[slot], y2_hbm.at[tile_rows(i), :], y2_sem.at[slot])

    def y2_load(i, slot):
        return pltpu.make_async_copy(y2_hbm.at[tile_rows(i), :], y2c.at[slot], yc_sem.at[slot])

    def y_store(i, slot):
        return pltpu.make_async_copy(yt.at[slot], y_hbm.at[tile_rows(i), :], yt_sem.at[slot])

    def start(copies):
        for cp in copies:
            cp.start()

    def side_by_side(count, one):
        def body(i, _):
            for u in range(UNROLL):
                one(i * UNROLL + u)
            return 0

        lax.fori_loop(0, count // UNROLL, body, 0)

    def all_of(c):
        return pl.ds(c * pc, pc)

    def lo_of(c):
        return pl.ds(c * pc, ph)

    def hi_of(c):
        return pl.ds(c * pc + ph, ph)

    def rs(kind, g, c):
        ss, rr = rs_s.at[kind, g, c], rs_r.at[kind, g, c]
        mine = part.at[g, core]
        if kind == D2D:
            return rdma(part.at[g, 1 - core, :, all_of(c)], dbuf.at[g, :, all_of(c)], ss, rr, mate)
        if kind == TUP:
            return rdma(mine.at[cop, lo_of(c)], tbuf.at[0, g, pl.ds(c * ph, ph)], ss, rr, up)
        if kind == TDN:
            return rdma(mine.at[cop, hi_of(c)], tbuf.at[1, g, pl.ds(c * ph, ph)], ss, rr, dn)
        if kind == RUP:
            return rdma(mine.at[cup, hi_of(c)], rbuf.at[0, g, hi_of(c)], ss, rr, up)
        if kind == RDN:
            return rdma(mine.at[cdn, lo_of(c)], rbuf.at[1, g, lo_of(c)], ss, rr, dn)
        if kind == SUP:
            return rdma(mine.at[cup, lo_of(c)], rbuf.at[0, g, lo_of(c)], ss, rr, up)
        return rdma(mine.at[cdn, hi_of(c)], rbuf.at[1, g, hi_of(c)], ss, rr, dn)

    def stage1(g, c):
        rs(D2D, g, c).wait_recv()

        def body(i, _):
            q = c * pc + i
            a = part[g, core, :, q].astype(F32) + dbuf[g, :, q].astype(F32)
            part[g, core, :, q] = a.astype(BF16)
            return 0

        lax.fori_loop(0, pc, body, 0)
        for kind in (TUP, TDN, RUP, RDN):
            rs(kind, g, c).start()

    def stage2(g, c):
        for kind, nxt, dst, off, d in ((TUP, SUP, cup, 0, 0), (TDN, SDN, cdn, ph, 1)):
            rs(kind, g, c).wait_recv()

            def body(i, _):
                q = c * pc + off + i
                a = part[g, core, dst, q].astype(F32) + tbuf[d, g, c * ph + i].astype(F32)
                part[g, core, dst, q] = a.astype(BF16)
                return 0

            lax.fori_loop(0, ph, body, 0)
            rs(nxt, g, c).start()

    def stage3(g, c):
        for kind in (RUP, RDN, SUP, SDN):
            rs(kind, g, c).wait_recv()
        zg = zo[...]
        lane = lax.broadcasted_iota(jnp.int32, zg.shape, 1)

        def one(i):
            q = c * pc + i
            z = jnp.sum(jnp.where(lane == g * npair + q, zg, 0.0), axis=1, keepdims=True)
            a = part[g, core, chip, q].astype(F32) + rbuf[0, g, q].astype(F32) + rbuf[1, g, q].astype(F32)
            a = a / z
            for j in range(ntile):
                sbuf[j, pl.ds(pl.multiple_of(q * 16, 16), 16), :] = a[:, j * LANES:(j + 1) * LANES]

        side_by_side(pc, one)

    def run3(g):
        def body(c, _):
            stage3(g, c)
            return 0

        lax.fori_loop(0, NCHUNK, body, 0)

        def sent(c, _):
            for kind in range(7):
                rs(kind, g, c).wait_send()
            return 0

        lax.fori_loop(0, NCHUNK, sent, 0)
        for dev in (up, dn, mate):
            pl.semaphore_signal(free_sem.at[g], inc=1, device_id={'seq': dev}, device_id_type=MESH)

    def ag(kind, g, c):
        origin, part_of, dev = {OUP: (chip, all_of, up), ODN: (chip, all_of, dn), OPA: (chip, all_of, mate),
                                FUP: (cdn, lo_of, up), FDN: (cup, hi_of, dn),
                                PUP: (cdn, all_of, mate), PDN: (cup, all_of, mate),
                                PLO: (cop, lo_of, mate), PHI: (cop, hi_of, mate)}[kind]
        ref = part.at[g, core, origin, part_of(c)]
        return rdma(ref, ref, ag_s.at[kind, g, c], ag_r.at[kind, g, c], dev)

    def send_own(g, c):
        for kind in (OUP, ODN, OPA):
            ag(kind, g, c).start()

    def pack(g):
        def body(q, _):
            for j in range(ntile):
                part[g, core, chip, q, :, j * LANES:(j + 1) * LANES] = (
                    sbuf[j, pl.ds(pl.multiple_of(q * 16, 16), 16), :].astype(BF16))
            return 0

        lax.fori_loop(0, npair, body, 0)
        pl.semaphore_wait(free_sem.at[g], 3)

    def relay1(g, c):
        ag(OUP, g, c).wait_recv()
        ag(FUP, g, c).start()
        ag(PUP, g, c).start()
        ag(ODN, g, c).wait_recv()
        ag(FDN, g, c).start()
        ag(PDN, g, c).start()

    def relay2(g, c):
        ag(FUP, g, c).wait_recv()
        ag(PLO, g, c).start()
        ag(FDN, g, c).wait_recv()
        ag(PHI, g, c).start()

    def front(c):
        x_load(c).wait()

        @pl.when(c >= 2)
        def _():
            xn_store(c - 2).wait()

        first = me * tok

        def one(p):
            q = c * pc + p
            b, sl = w2_rows(c, p * rows, rows)
            x = w2b[b, sl, :].astype(F32)
            inv = lax.rsqrt(jnp.sum(x * x, axis=1, keepdims=True) + NORM_EPS)
            xn = (x * inv).astype(BF16)
            b, sl = w2_rows(NCHUNK + c % 2, p * rows, rows)
            w2b[b, sl, :] = xn
            logits = dot(xn, phi[...])
            ri = lax.broadcasted_iota(jnp.int32, (rows, cols), 0)
            ci = lax.broadcasted_iota(jnp.int32, (rows, cols), 1)
            odd = ri >= tok
            same = jnp.where(odd, 1, 0) == ((ci >> 3) & 1)
            lim = jnp.where(odd, len_ref[2 * q + 1], len_ref[2 * q])
            valid = (first + (ri & (tok - 1))) < lim
            own = jnp.where(same, logits, NEG_BIG)
            top = jnp.max(own, axis=1, keepdims=True)
            ex = jnp.exp(own - top)
            mixb[pl.ds(pl.multiple_of(q * rows, rows), rows), :] = (
                ex * (1.0 / jnp.sum(ex, axis=1, keepdims=True))).astype(BF16)
            lm = jnp.where(valid, own, NEG_BIG)
            lb[c % 2, pl.ds(pl.multiple_of(p * rows, rows), rows), :] = lm
            pm[pl.ds(q, 1), :] = jnp.max(lm, axis=0, keepdims=True)

        side_by_side(pc, one)
        xn_store(c).start()

    def mx_msg(k, c):
        sl = pl.ds(pl.multiple_of(c * pc, pc), pc)
        return rdma(pm.at[sl, :], mxb.at[me, sl, :], mx_s.at[k - 1, c], mx_r.at[k - 1, c], lax.rem(me + k, n))

    half = cols // 2

    def numerators(c):
        sl = pl.ds(pl.multiple_of(c * pc, pc), pc)
        for k in range(1, n):
            mx_msg(k, c).wait_recv()
        top = pm[sl, :]
        for k in range(1, n):
            top = jnp.maximum(top, mxb[lax.rem(me + n - k, n), sl, :])
        mx[sl, :] = top

        def one(p):
            q = c * pc + p
            e = jnp.exp(lb[c % 2, pl.ds(pl.multiple_of(p * rows, rows), rows), :] - mx[pl.ds(q, 1), :])
            z = jnp.sum(e, axis=0, keepdims=True)
            zs[pl.ds(q, 1), :] = z[:, :half]
            zs[pl.ds(npair + q, 1), :] = z[:, half:]
            b, xsl = w2_rows(c, p * rows, rows)
            num = lax.dot_general(e.astype(BF16), w2b[b, xsl, :], (((0,), (0,)), ((), ())),
                                  preferred_element_type=F32)
            part[:, :, :, q] = num.astype(BF16).reshape(NGRP, 2, chips, 16, dwidth)

        side_by_side(pc, one)
        for g in range(NGRP):
            rs(D2D, g, c).start()

    def dense_tile(i):
        slot = i % 2
        xn_load(i, slot).wait()
        xt = xnb[slot]
        hidden = wsi.shape[1]
        step = min(hidden, 768)
        acc = None
        for f in range(0, hidden, step):
            h = gelu(dot(xt, wsi[:, f:f + step])).astype(BF16)
            o = dot(h, wso[f:f + step, :])
            acc = o if acc is None else acc + o

        @pl.when(i >= 2)
        def _():
            y2_store(i - 2, slot).wait()

        y2b[slot] = acc
        y2_store(i, slot).start()

        @pl.when(i + 2 < dtiles)
        def _():
            xn_load(i + 2, slot).start()

    def expert(g, e, total):
        idx = g * ER + e
        slot = idx % 2
        xin = jnp.concatenate([sbuf[j, pl.ds(e, 2 * npair, stride=ER), :] for j in range(ntile)], axis=1).astype(BF16)
        l1, l2 = w_load(idx, slot)
        l1.wait()
        l2.wait()
        hidden = w1b.shape[2]
        step = min(hidden, 768)
        acc = None
        for f in range(0, hidden, step):
            h = gelu(dot(xin, w1b[slot, :, f:f + step])).astype(BF16)
            o = dot(h, w2b[slot, f:f + step, :])
            acc = o if acc is None else acc + o
        for j in range(ntile):
            sbuf[j, pl.ds(e, 2 * npair, stride=ER), :] = acc[:, j * LANES:(j + 1) * LANES]

        @pl.when(idx + 2 < total)
        def _():
            start(w_load(idx + 2, slot))

    def combine(c):
        tiles = crows // DTOK
        first = c * tiles
        y2_load(first, 0).start()
        y2_load(first + 1, 1).start()
        for g in range(NGRP):
            for kind in (OPA, PUP, PDN, PLO, PHI):
                ag(kind, g, c).wait_recv()
        for t in range(tiles):
            i, slot = first + t, t % 2
            y2_load(i, slot).wait()
            if c > 0 or t >= 2:
                y_store(i - 2, slot).wait()
            for u in range(DTOK // rows):
                q = i * (DTOK // rows) + u
                lr = slice(u * rows, (u + 1) * rows)
                rhs = part[:, :, :, q].reshape(cols, dwidth)
                yt[slot, lr, :] = (dot(mixb[q * rows:(q + 1) * rows, :], rhs) + y2c[slot, lr, :]).astype(BF16)
            y_store(i, slot).start()
            if t + 2 < tiles:
                y2_load(i + 2, slot).start()

    for c in range(NCHUNK):
        x_load(c).start()
    start(ws_load())
    barrier = pltpu.get_barrier_semaphore()
    for k in range(1, n):
        pl.semaphore_signal(barrier, inc=1, device_id={'seq': lax.rem(me + k, n)}, device_id_type=MESH)
    zs[...] = jnp.zeros_like(zs)
    pl.semaphore_wait(barrier, n - 1)

    def opening(s, _):
        @pl.when(s < NCHUNK)
        def _():
            front(s)
            for k in range(1, n):
                mx_msg(k, s).start()

        @pl.when(s == 2)
        def _():
            xn_load(0, 0).start()
            xn_load(1, 1).start()

        @pl.when(s == NCHUNK)
        def _():
            for cp in ws_load():
                cp.wait()

        @pl.when(s >= NCHUNK)
        def _():
            dense_tile(s - NCHUNK)

        @pl.when(s >= 2)
        def _():
            stage1(0, s - 2)

        @pl.when((s >= 1) & (s <= NCHUNK))
        def _():
            numerators(s - 1)

        return 0

    lax.fori_loop(0, NCHUNK + 2, opening, 0)
    for c in (NCHUNK - 2, NCHUNK - 1):
        xn_store(c).wait()
    start(w_load(0, 0))
    start(w_load(1, 1))

    zt[...] = zs[...].T.reshape(zt.shape)

    def z_msg(k):
        dev = lax.rem(me + k, n)
        return rdma(zt.at[dev % 2, dev // 2], zb.at[me], z_s.at[k - 1], z_r.at[k - 1], dev)

    for k in range(1, n):
        z_msg(k).start()

    def dense_a(i, _):
        dense_tile(2 + i)

        @pl.when(i < NCHUNK)
        def _():
            stage2(0, i)

        return 0

    lax.fori_loop(0, DENSE_A - 2, dense_a, 0)

    def next1(c, _):
        stage1(1, c)
        return 0

    lax.fori_loop(0, NCHUNK, next1, 0)
    for k in range(1, n):
        z_msg(k).wait_recv()
    ztot = zt[core, chip]
    for k in range(1, n):
        ztot = ztot + zb[lax.rem(me + n - k, n)]
    zo[...] = ztot
    run3(0)

    total = NGRP * ER

    def experts_a(e, _):
        expert(0, e, total)

        @pl.when(e < NCHUNK)
        def _():
            stage2(1, e)

        for k, at in enumerate(DENSE_E):
            @pl.when(e == at)
            def _():
                dense_tile(DENSE_A + k)

        return 0

    lax.fori_loop(0, ER, experts_a, 0)
    pack(0)
    for c in range(NCHUNK):
        send_own(0, c)
    run3(1)

    def experts_b(e, _):
        expert(1, e, total)

        @pl.when(e < NCHUNK)
        def _():
            relay1(0, e)

        @pl.when(e >= NCHUNK)
        def _():
            relay2(0, e - NCHUNK)

        for k, at in enumerate(DENSE_E):
            @pl.when(e == at)
            def _():
                dense_tile(DENSE_A + len(DENSE_E) + k)

        return 0

    lax.fori_loop(0, ER, experts_b, 0)
    pack(1)
    send_own(1, 0)
    send_own(1, 1)

    before = DENSE_A + 2 * len(DENSE_E)
    count = dtiles - before
    events = ((2, relay1, 0), (2, send_own, 2), (4, relay1, 1), (4, send_own, 3), (5, relay2, 0),
              (7, relay1, 2), (7, relay2, 1), (8, None, 0), (99, relay1, 3), (99, relay2, 2), (99, None, 1), (99, None, 2),
              (99, relay2, 3), (99, None, 3))

    def run(at, what, c):
        if what is None:
            combine(c)
        else:
            what(1, c)

    def dense_b(i, _):
        dense_tile(before + i)
        for at, what, c in events:
            if at < count:
                @pl.when(i == at)
                def _():
                    run(at, what, c)
        return 0

    lax.fori_loop(0, count, dense_b, 0)
    y2_store(dtiles - 2, (dtiles - 2) % 2).wait()
    y2_store(dtiles - 1, (dtiles - 1) % 2).wait()
    for at, what, c in events:
        if at >= count:
            run(at, what, c)

    y_store(dtiles - 2, 0).wait()
    y_store(dtiles - 1, 1).wait()
    for k in range(1, n):
        z_msg(k).wait_send()

    def drain(c, _):
        for k in range(1, n):
            mx_msg(k, c).wait_send()
        for g in range(NGRP):
            for kind in range(9):
                ag(kind, g, c).wait_send()
        return 0

    lax.fori_loop(0, NCHUNK, drain, 0)


def solution(mesh):
    n = mesh.shape['seq']
    chips = n // 2
    tok_spec = P('data', 'seq', None)
    expert_spec = P('seq', None, None)

    def per_device(x_blk, len_blk, phi_slots, scale_g, w_in_blk, w_out_blk, ws_in, ws_out):
        batch, tok, width = x_blk.shape
        slots = phi_slots.shape[1]
        hidden = ws_in.shape[1]
        cols = 2 * slots
        npair = batch // 2
        ntok = batch * tok
        x2 = x_blk.reshape(ntok, width)
        phi_norm = (scale_g * unit_rows(phi_slots, 0)).astype(BF16)
        phi_cols = phi_norm.reshape(width, chips, 2, NGRP, ER).transpose(0, 3, 2, 1, 4)
        phi_cols = jnp.broadcast_to(phi_cols[:, :, :, :, None, :], (width, NGRP, 2, chips, 2, ER)).reshape(width, cols)

        pc = npair // NCHUNK
        rows = 2 * tok
        any_spec = pl.BlockSpec(memory_space=pl.ANY)
        sem = pltpu.SemaphoreType.DMA
        y, _, _ = pl.pallas_call(
            functools.partial(mega_kernel, n, tok),
            in_specs=[pl.BlockSpec(memory_space=pltpu.SMEM), pl.BlockSpec(memory_space=pltpu.VMEM),
                      any_spec, any_spec, any_spec, any_spec, any_spec],
            out_specs=[any_spec, any_spec, any_spec],
            out_shape=[jax.ShapeDtypeStruct((ntok, width), BF16),
                       jax.ShapeDtypeStruct((ntok, width), F32),
                       jax.ShapeDtypeStruct((ntok, width), BF16)],
            scratch_shapes=[
                pltpu.VMEM((NGRP, 2, chips, npair, 16, width), BF16),
                pltpu.VMEM((NGRP, chips, npair, 16, width), BF16),
                pltpu.VMEM((2, NGRP, npair // 2, 16, width), BF16),
                pltpu.VMEM((2, NGRP, npair, 16, width), BF16),
                pltpu.VMEM((width, hidden), BF16),
                pltpu.VMEM((hidden, width), BF16),
                pltpu.VMEM((2, width, hidden), BF16),
                pltpu.VMEM((2, hidden, width), BF16),
                pltpu.VMEM((2, pc * rows, cols), F32),
                pltpu.VMEM((ntok, cols), BF16),
                pltpu.VMEM((2, DTOK, width), BF16),
                pltpu.VMEM((2, DTOK, width), F32),
                pltpu.VMEM((2, DTOK, width), F32),
                pltpu.VMEM((2, DTOK, width), BF16),
                pltpu.VMEM((width // LANES, npair * 16, LANES), F32),
                pltpu.VMEM((npair, cols), F32),
                pltpu.VMEM((n, npair, cols), F32),
                pltpu.VMEM((npair, cols), F32),
                pltpu.VMEM((LANES, cols // 2), F32),
                pltpu.VMEM((2, chips, 16, LANES), F32),
                pltpu.VMEM((n, 16, LANES), F32),
                pltpu.VMEM((16, LANES), F32),
                sem((7, NGRP, NCHUNK)), sem((7, NGRP, NCHUNK)),
                sem((9, NGRP, NCHUNK)), sem((9, NGRP, NCHUNK)),
                sem((n - 1, NCHUNK)), sem((n - 1, NCHUNK)), sem((n - 1,)), sem((n - 1,)),
                sem((NCHUNK,)), sem((2,)), sem((2,)), sem((2, 2)), sem((2,)), sem((2,)),
                sem((2,)), sem((2,)), pltpu.SemaphoreType.REGULAR((NGRP,)),
            ],
            compiler_params=pltpu.CompilerParams(collective_id=0, has_side_effects=True,
                                                 vmem_limit_bytes=VMEM_BYTES),
            name='mega',
        )(len_blk, phi_cols, x2, ws_in, ws_out, w_in_blk, w_out_blk)
        return y.reshape(batch, tok, width)

    return jax.shard_map(per_device, mesh=mesh, in_specs=(tok_spec, P('data'), P(), P(), expert_spec, expert_spec, P(), P()), out_specs=tok_spec, check_vma=False)
```

time: 176 us -> 161 us (0.915)
  Pallas kernels: 173 us -> 152 us
  local copies, waits for them, and re-layouts: 2.01 us -> 8.26 us
    pallas_call x3 -> x1, Pallas kernels: 173 us -> 152 us  [per_device(): pl.pallas_call(functools.partial(mega_kernel, n, tok), in_specs=[pl.Block...]
    unnamed x1 -> x2, local copies, waits for them, and re-layouts: 1.06 us -> 7.3 us
where the time goes in v1:
time: 161 us
  Pallas kernels  152 us (94%)
  local copies, waits for them, and re-layouts  8.26 us (5%)
    pallas_call x1, Pallas kernels, per_device(): pl.pallas_call(functools.partial(mega_kernel, n, tok), in_specs=[pl.Block...  152 us
    unnamed x2, local copies, waits for them, and re-layouts  7.3 us

profile of v1, /device:TPU:113, one launch (start us, length us, event | category | flops | bytes accessed | tf_op | source)
XLA Modules:
  0.0 161.0 jit_solution(8180225518303976093)
XLA Ops:
  0.7 1.1 copy.10
  1.7 0.1 fusion
  1.8 0.1 fusion.2
  2.0 0.9 copy.12.phi
  3.0 151.8 %mega.1 = (bf16[4096,768]{1,0:T(8,128)(2,1)}, f32[4096,768]{1,0:T(8,128)}, bf16[4096,768]{1,0:T(8,128)(2,1)}) custom-call(s32[64]{0:T(128)} %len_ref.1, bf16[768,256]{1,0:T(8,128)(2,1)} %copy.12.phi, bf16[4096,768]{1,0:T(8,128)(2,1)} %bitcast.6, bf16[768,3072]{1,0:T(8,128)(2,1)} %wsi_hbm.1, bf16[3072,768]{1,0:T(8,128)(2,1)} %wso_hbm.1, ...), custom_call_target="tpu_custom_call" | custom-call | tf_op jit(solution)/shard_map/mega/pallas_call | solution.py:559
  154.7 6.2 %copy.15 = bf16[64,64,768]{2,1,0:T(8,128)(2,1)} copy(bf16[64,64,768]{2,1,0:T(8,128)(2,1)} %bitcast.7) | data formatting | bytes 12582912
  (3 shorter events, 0.1 us)

commit v2 on v1

--- a/solution.py
+++ b/solution.py
@@ -2,6 +2,7 @@
 
 import jax
 import jax.numpy as jnp
+import numpy as np
 from jax import lax
 from jax.experimental import pallas as pl
 from jax.experimental.pallas import tpu as pltpu
@@ -19,8 +20,7 @@
 VMEM_BYTES = 67043328
 UNROLL = 4
 DTOK = 256
-DENSE_A = 6
-DENSE_E = ()
+DENSE_A = 5
 
 D2D, TUP, TDN, RUP, RDN, SUP, SDN = range(7)
 OUP, ODN, OPA, FUP, FDN, PUP, PDN, PLO, PHI = range(9)
@@ -39,10 +39,10 @@
     return jax.nn.gelu(v, approximate=True)
 
 
-def mega_kernel(n, tok, len_ref, phi, x_hbm, wsi_hbm, wso_hbm, w1_hbm, w2_hbm,
+def mega_kernel(n, tok, len_ref, gain_ref, phi_ref, perm_ref, x_hbm, wsi_hbm, wso_hbm, w1_hbm, w2_hbm,
                 y_hbm, y2_hbm, xn_hbm,
-                part, dbuf, tbuf, rbuf, wsi, wso, w1b, w2b, lb, mixb, xnb, y2b, y2c, yt, sbuf,
-                pm, mxb, mx, zs, zt, zb, zo,
+                part, dbuf, tbuf, rbuf, wsi, wso, w1b, w2b, mixb, xnb, y2b, y2c, yt, sbuf,
+                phi, pm, mxb, mx, zs, zt, zb, zo,
                 rs_s, rs_r, ag_s, ag_r, mx_s, mx_r, z_s, z_r, x_sem, xs_sem, ws_sem, w_sem, xn_sem, y2_sem,
                 yc_sem, yt_sem, free_sem):
     me = lax.axis_index('seq')
@@ -57,6 +57,7 @@
     rows = 2 * tok
     crows = pc * rows
     dwidth = phi.shape[0]
+    tiles = crows // DTOK
     ntile = dwidth // LANES
     dtiles = y2_hbm.shape[0] // DTOK
     per = w2b.shape[1] // crows
@@ -233,6 +234,11 @@
         ag(PLO, g, c).start()
         ag(FDN, g, c).wait_recv()
         ag(PHI, g, c).start()
+
+    def logit_at(c, p):
+        each = DTOK // rows
+        return (p // each, pl.ds(pl.multiple_of(p % each * rows, rows), rows),
+                pl.ds(pl.multiple_of(c % (NCHUNK - 1) * cols, cols), cols))
 
     def front(c):
         x_load(c).wait()
@@ -264,7 +270,8 @@
             mixb[pl.ds(pl.multiple_of(q * rows, rows), rows), :] = (
                 ex * (1.0 / jnp.sum(ex, axis=1, keepdims=True))).astype(BF16)
             lm = jnp.where(valid, own, NEG_BIG)
-            lb[c % 2, pl.ds(pl.multiple_of(p * rows, rows), rows), :] = lm
+            t, tr, tc = logit_at(c, p)
+            y2c[t, tr, tc] = lm
             pm[pl.ds(q, 1), :] = jnp.max(lm, axis=0, keepdims=True)
 
         side_by_side(pc, one)
@@ -287,7 +294,8 @@
 
         def one(p):
             q = c * pc + p
-            e = jnp.exp(lb[c % 2, pl.ds(pl.multiple_of(p * rows, rows), rows), :] - mx[pl.ds(q, 1), :])
+            t, tr, tc = logit_at(c, p)
+            e = jnp.exp(y2c[t, tr, tc] - mx[pl.ds(q, 1), :])
             z = jnp.sum(e, axis=0, keepdims=True)
             zs[pl.ds(q, 1), :] = z[:, :half]
             zs[pl.ds(npair + q, 1), :] = z[:, half:]
@@ -344,27 +352,26 @@
         def _():
             start(w_load(idx + 2, slot))
 
-    def combine(c):
-        tiles = crows // DTOK
-        first = c * tiles
-        y2_load(first, 0).start()
-        y2_load(first + 1, 1).start()
+    def prefetch(_, c):
+        for t in range(tiles):
+            y2_load(c * tiles + t, t).start()
+
+    def combine(_, c):
         for g in range(NGRP):
             for kind in (OPA, PUP, PDN, PLO, PHI):
                 ag(kind, g, c).wait_recv()
         for t in range(tiles):
-            i, slot = first + t, t % 2
-            y2_load(i, slot).wait()
-            if c > 0 or t >= 2:
-                y_store(i - 2, slot).wait()
-            for u in range(DTOK // rows):
-                q = i * (DTOK // rows) + u
-                lr = slice(u * rows, (u + 1) * rows)
-                rhs = part[:, :, :, q].reshape(cols, dwidth)
-                yt[slot, lr, :] = (dot(mixb[q * rows:(q + 1) * rows, :], rhs) + y2c[slot, lr, :]).astype(BF16)
-            y_store(i, slot).start()
-            if t + 2 < tiles:
-                y2_load(i + 2, slot).start()
+            y2_load(c * tiles + t, t).wait()
+            if c > 0:
+                y_store((c - 1) * tiles + t, t).wait()
+        for p in range(pc):
+            q = c * pc + p
+            t, off = p * rows // DTOK, p * rows % DTOK
+            rhs = part[:, :, :, q].reshape(cols, dwidth)
+            yt[t, off:off + rows, :] = (dot(mixb[q * rows:(q + 1) * rows, :], rhs)
+                                        + y2c[t, off:off + rows, :]).astype(BF16)
+        for t in range(tiles):
+            y_store(c * tiles + t, t).start()
 
     for c in range(NCHUNK):
         x_load(c).start()
@@ -373,44 +380,40 @@
     for k in range(1, n):
         pl.semaphore_signal(barrier, inc=1, device_id={'seq': lax.rem(me + k, n)}, device_id_type=MESH)
     zs[...] = jnp.zeros_like(zs)
-    pl.semaphore_wait(barrier, n - 1)
-
-    def opening(s, _):
-        @pl.when(s < NCHUNK)
+    phi[...] = dot((gain_ref[0] * unit_rows(phi_ref[...], 0)).astype(BF16), perm_ref[...]).astype(BF16)
+
+    def openings(s, _):
+        front(s)
+
+        @pl.when(s == 0)
         def _():
-            front(s)
-            for k in range(1, n):
-                mx_msg(k, s).start()
-
-        @pl.when(s == 2)
-        def _():
-            xn_load(0, 0).start()
-            xn_load(1, 1).start()
-
-        @pl.when(s == NCHUNK)
-        def _():
-            for cp in ws_load():
-                cp.wait()
-
-        @pl.when(s >= NCHUNK)
-        def _():
-            dense_tile(s - NCHUNK)
-
-        @pl.when(s >= 2)
-        def _():
-            stage1(0, s - 2)
-
-        @pl.when((s >= 1) & (s <= NCHUNK))
-        def _():
-            numerators(s - 1)
-
+            pl.semaphore_wait(barrier, n - 1)
+
+        for k in range(1, n):
+            mx_msg(k, s).start()
         return 0
 
-    lax.fori_loop(0, NCHUNK + 2, opening, 0)
+    lax.fori_loop(0, NCHUNK - 1, openings, 0)
+    xn_load(0, 0).start()
+    xn_load(1, 1).start()
+    numerators(0)
+    front(NCHUNK - 1)
+    for k in range(1, n):
+        mx_msg(k, NCHUNK - 1).start()
+    stage1(0, 0)
+    numerators(1)
+
+    def more(c, _):
+        numerators(c)
+        stage1(0, c - 1)
+        return 0
+
+    lax.fori_loop(2, NCHUNK, more, 0)
     for c in (NCHUNK - 2, NCHUNK - 1):
         xn_store(c).wait()
     start(w_load(0, 0))
     start(w_load(1, 1))
+    stage2(0, 0)
 
     zt[...] = zs[...].T.reshape(zt.shape)
 
@@ -421,22 +424,32 @@
     for k in range(1, n):
         z_msg(k).start()
 
-    def dense_a(i, _):
-        dense_tile(2 + i)
-
-        @pl.when(i < NCHUNK)
-        def _():
-            stage2(0, i)
-
-        return 0
-
-    lax.fori_loop(0, DENSE_A - 2, dense_a, 0)
-
-    def next1(c, _):
-        stage1(1, c)
-        return 0
-
-    lax.fori_loop(0, NCHUNK, next1, 0)
+    for cp in ws_load():
+        cp.wait()
+
+    def steps(count, one, events):
+        def body(i, _):
+            one(i)
+            for at, what, g, c in events:
+                if at < count:
+                    @pl.when(i == at)
+                    def _():
+                        what(g, c)
+            return 0
+
+        lax.fori_loop(0, count, body, 0)
+        for at, what, g, c in events:
+            if at >= count:
+                what(g, c)
+
+    def dense_at(_, i):
+        dense_tile(i)
+
+    stage1(0, NCHUNK - 1)
+    stage2(0, 1)
+
+    steps(DENSE_A, dense_tile, ((0, stage2, 0, 2), (2, stage2, 0, 3), (2, stage1, 1, 0), (3, stage1, 1, 1),
+                                (3, stage1, 1, 2), (3, stage1, 1, 3)))
     for k in range(1, n):
         z_msg(k).wait_recv()
     ztot = zt[core, chip]
@@ -446,80 +459,37 @@
     run3(0)
 
     total = NGRP * ER
-
-    def experts_a(e, _):
-        expert(0, e, total)
-
-        @pl.when(e < NCHUNK)
-        def _():
-            stage2(1, e)
-
-        for k, at in enumerate(DENSE_E):
-            @pl.when(e == at)
-            def _():
-                dense_tile(DENSE_A + k)
-
-        return 0
-
-    lax.fori_loop(0, ER, experts_a, 0)
+    steps(ER, lambda e: expert(0, e, total),
+          ((1, stage2, 1, 0), (1, dense_at, 0, DENSE_A), (3, stage2, 1, 1), (4, stage2, 1, 2),
+           (5, dense_at, 0, DENSE_A + 1), (5, stage2, 1, 3)))
     pack(0)
     for c in range(NCHUNK):
         send_own(0, c)
     run3(1)
 
-    def experts_b(e, _):
-        expert(1, e, total)
-
-        @pl.when(e < NCHUNK)
-        def _():
-            relay1(0, e)
-
-        @pl.when(e >= NCHUNK)
-        def _():
-            relay2(0, e - NCHUNK)
-
-        for k, at in enumerate(DENSE_E):
-            @pl.when(e == at)
-            def _():
-                dense_tile(DENSE_A + len(DENSE_E) + k)
-
-        return 0
-
-    lax.fori_loop(0, ER, experts_b, 0)
+    steps(ER, lambda e: expert(1, e, total),
+          ((1, dense_at, 0, DENSE_A + 2), (1, relay1, 0, 0), (3, relay1, 0, 1), (5, relay1, 0, 2),
+           (5, dense_at, 0, DENSE_A + 3), (5, relay1, 0, 3)))
     pack(1)
     send_own(1, 0)
     send_own(1, 1)
 
-    before = DENSE_A + 2 * len(DENSE_E)
-    count = dtiles - before
-    events = ((2, relay1, 0), (2, send_own, 2), (4, relay1, 1), (4, send_own, 3), (5, relay2, 0),
-              (7, relay1, 2), (7, relay2, 1), (8, None, 0), (99, relay1, 3), (99, relay2, 2), (99, None, 1), (99, None, 2),
-              (99, relay2, 3), (99, None, 3))
-
-    def run(at, what, c):
-        if what is None:
-            combine(c)
-        else:
-            what(1, c)
-
-    def dense_b(i, _):
-        dense_tile(before + i)
-        for at, what, c in events:
-            if at < count:
-                @pl.when(i == at)
-                def _():
-                    run(at, what, c)
-        return 0
-
-    lax.fori_loop(0, count, dense_b, 0)
-    y2_store(dtiles - 2, (dtiles - 2) % 2).wait()
-    y2_store(dtiles - 1, (dtiles - 1) % 2).wait()
-    for at, what, c in events:
-        if at >= count:
-            run(at, what, c)
-
-    y_store(dtiles - 2, 0).wait()
-    y_store(dtiles - 1, 1).wait()
+    before = DENSE_A + 4
+    steps(dtiles - before, lambda i: dense_tile(before + i),
+          ((0, relay2, 0, 0), (0, relay2, 0, 1), (0, relay2, 0, 2), (0, relay2, 0, 3), (0, prefetch, 0, 0),
+           (1, relay1, 1, 0), (1, send_own, 1, 2),
+           (3, relay1, 1, 1), (3, send_own, 1, 3), (4, relay2, 1, 0), (5, relay1, 1, 2), (5, combine, 0, 0),
+           (5, prefetch, 0, 1), (6, relay2, 1, 1), (6, combine, 0, 1), (6, prefetch, 0, 2), (6, relay1, 1, 3)))
+    for i in (dtiles - 2, dtiles - 1):
+        y2_store(i, i % 2).wait()
+    relay2(1, 2)
+    combine(0, 2)
+    prefetch(0, 3)
+    relay2(1, 3)
+    combine(0, 3)
+
+    for t in range(tiles):
+        y_store(dtiles - tiles + t, t).wait()
     for k in range(1, n):
         z_msg(k).wait_send()
 
@@ -548,9 +518,9 @@
         npair = batch // 2
         ntok = batch * tok
         x2 = x_blk.reshape(ntok, width)
-        phi_norm = (scale_g * unit_rows(phi_slots, 0)).astype(BF16)
-        phi_cols = phi_norm.reshape(width, chips, 2, NGRP, ER).transpose(0, 3, 2, 1, 4)
-        phi_cols = jnp.broadcast_to(phi_cols[:, :, :, :, None, :], (width, NGRP, 2, chips, 2, ER)).reshape(width, cols)
+        col = np.arange(cols)
+        slot = ((col // 16 % chips * 2 + col // (16 * chips) % 2) * NGRP + col // (32 * chips)) * ER + col % ER
+        perm = jnp.asarray(np.arange(slots)[:, None] == slot[None, :], BF16)
 
         pc = npair // NCHUNK
         rows = 2 * tok
@@ -558,7 +528,8 @@
         sem = pltpu.SemaphoreType.DMA
         y, _, _ = pl.pallas_call(
             functools.partial(mega_kernel, n, tok),
-            in_specs=[pl.BlockSpec(memory_space=pltpu.SMEM), pl.BlockSpec(memory_space=pltpu.VMEM),
+            in_specs=[pl.BlockSpec(memory_space=pltpu.SMEM), pl.BlockSpec(memory_space=pltpu.SMEM),
+                      pl.BlockSpec(memory_space=pltpu.VMEM), pl.BlockSpec(memory_space=pltpu.VMEM),
                       any_spec, any_spec, any_spec, any_spec, any_spec],
             out_specs=[any_spec, any_spec, any_spec],
             out_shape=[jax.ShapeDtypeStruct((ntok, width), BF16),
@@ -573,13 +544,13 @@
                 pltpu.VMEM((hidden, width), BF16),
                 pltpu.VMEM((2, width, hidden), BF16),
                 pltpu.VMEM((2, hidden, width), BF16),
-                pltpu.VMEM((2, pc * rows, cols), F32),
                 pltpu.VMEM((ntok, cols), BF16),
                 pltpu.VMEM((2, DTOK, width), BF16),
                 pltpu.VMEM((2, DTOK, width), F32),
-                pltpu.VMEM((2, DTOK, width), F32),
-                pltpu.VMEM((2, DTOK, width), BF16),
+                pltpu.VMEM((pc * rows // DTOK, DTOK, width), F32),
+                pltpu.VMEM((pc * rows // DTOK, DTOK, width), BF16),
                 pltpu.VMEM((width // LANES, npair * 16, LANES), F32),
+                pltpu.VMEM((width, cols), BF16),
                 pltpu.VMEM((npair, cols), F32),
                 pltpu.VMEM((n, npair, cols), F32),
                 pltpu.VMEM((npair, cols), F32),
@@ -591,12 +562,12 @@
                 sem((9, NGRP, NCHUNK)), sem((9, NGRP, NCHUNK)),
                 sem((n - 1, NCHUNK)), sem((n - 1, NCHUNK)), sem((n - 1,)), sem((n - 1,)),
                 sem((NCHUNK,)), sem((2,)), sem((2,)), sem((2, 2)), sem((2,)), sem((2,)),
-                sem((2,)), sem((2,)), pltpu.SemaphoreType.REGULAR((NGRP,)),
+                sem((pc * rows // DTOK,)), sem((pc * rows // DTOK,)), pltpu.SemaphoreType.REGULAR((NGRP,)),
             ],
             compiler_params=pltpu.CompilerParams(collective_id=0, has_side_effects=True,
                                                  vmem_limit_bytes=VMEM_BYTES),
             name='mega',
-        )(len_blk, phi_cols, x2, ws_in, ws_out, w_in_blk, w_out_blk)
+        )(len_blk, scale_g.reshape(1), phi_slots, perm, x2, ws_in, ws_out, w_in_blk, w_out_blk)
         return y.reshape(batch, tok, width)
 
     return jax.shard_map(per_device, mesh=mesh, in_specs=(tok_spec, P('data'), P(), P(), expert_spec, expert_spec, P(), P()), out_specs=tok_spec, check_vma=False)

time: 161 us -> 138 us (0.86)
  Pallas kernels: 152 us -> 131 us
  local copies, waits for them, and re-layouts: 8.26 us -> 6.24 us
    pallas_call x1, Pallas kernels: 152 us -> 131 us  [per_device(): pl.pallas_call(functools.partial(mega_kernel, n, tok), in_specs=[pl.Block...]
    unnamed x2 -> x1, local copies, waits for them, and re-layouts: 7.3 us -> 6.24 us
where the time goes in v2:
time: 138 us
  Pallas kernels  131 us (95%)
  local copies, waits for them, and re-layouts  6.24 us (5%)
    pallas_call x1, Pallas kernels, per_device(): pl.pallas_call(functools.partial(mega_kernel, n, tok), in_specs=[pl.Block...  131 us
    unnamed x1, local copies, waits for them, and re-layouts  6.24 us

profile of v2, /device:TPU:113, one launch (start us, length us, event | category | flops | bytes accessed | tf_op | source)
XLA Modules:
  0.0 138.2 jit_solution(16992546220831040921)
XLA Ops:
  0.7 131.3 %mega.1 = (bf16[4096,768]{1,0:T(8,128)(2,1)}, f32[4096,768]{1,0:T(8,128)}, bf16[4096,768]{1,0:T(8,128)(2,1)}) custom-call(s32[64]{0:T(128)} %len_ref.1, f32[1]{0:T(128)} %bitcast.3.gain_ref, bf16[768,128]{1,0:T(8,128)(2,1)} %phi_ref.1, bf16[128,256]{1,0:T(8,128)(2,1)} %constant.2.clone.perm_ref, bf16[4096,768]{1,0:T(8,128)(2,1)} %bitcast.4, ...), custom_call_target="tpu_custom_call" | custom-call | tf_op jit(solution)/shard_map/mega/pallas_call | solution.py:529
  132.0 6.2 %copy.12 = bf16[64,64,768]{2,1,0:T(8,128)(2,1)} copy(bf16[64,64,768]{2,1,0:T(8,128)(2,1)} %bitcast.5) | data formatting | bytes 12582912

commit v3 on v2

--- a/solution.py
+++ b/solution.py
@@ -40,11 +40,11 @@
 
 
 def mega_kernel(n, tok, len_ref, gain_ref, phi_ref, perm_ref, x_hbm, wsi_hbm, wso_hbm, w1_hbm, w2_hbm,
-                y_hbm, y2_hbm, xn_hbm,
-                part, dbuf, tbuf, rbuf, wsi, wso, w1b, w2b, mixb, xnb, y2b, y2c, yt, sbuf,
+                y_ref, y2_hbm, xn_hbm,
+                part, dbuf, tbuf, rbuf, wsi, wso, w1b, w2b, mixb, xnb, y2b, y2c,
                 phi, pm, mxb, mx, zs, zt, zb, zo,
                 rs_s, rs_r, ag_s, ag_r, mx_s, mx_r, z_s, z_r, x_sem, xs_sem, ws_sem, w_sem, xn_sem, y2_sem,
-                yc_sem, yt_sem, free_sem):
+                yc_sem, free_sem):
     me = lax.axis_index('seq')
     chip, core = me // 2, me % 2
     chips = n // 2
@@ -59,7 +59,7 @@
     dwidth = phi.shape[0]
     tiles = crows // DTOK
     ntile = dwidth // LANES
-    dtiles = y2_hbm.shape[0] // DTOK
+    dtiles = y2_hbm.shape[1] // DTOK
     per = w2b.shape[1] // crows
 
     def rdma(src, dst, ss, rs, dev):
@@ -94,14 +94,11 @@
     def xn_load(i, slot):
         return pltpu.make_async_copy(xn_hbm.at[tile_rows(i), :], xnb.at[slot], xn_sem.at[slot])
 
-    def y2_store(i, slot):
-        return pltpu.make_async_copy(y2b.at[slot], y2_hbm.at[tile_rows(i), :], y2_sem.at[slot])
+    def y2_store(i):
+        return pltpu.make_async_copy(y2b, y2_hbm.at[:, tile_rows(i), :], y2_sem)
 
     def y2_load(i, slot):
-        return pltpu.make_async_copy(y2_hbm.at[tile_rows(i), :], y2c.at[slot], yc_sem.at[slot])
-
-    def y_store(i, slot):
-        return pltpu.make_async_copy(yt.at[slot], y_hbm.at[tile_rows(i), :], yt_sem.at[slot])
+        return pltpu.make_async_copy(y2_hbm.at[:, tile_rows(i), :], y2c.at[:, tile_rows(slot), :], yc_sem.at[slot])
 
     def start(copies):
         for cp in copies:
@@ -123,6 +120,12 @@
 
     def hi_of(c):
         return pl.ds(c * pc + ph, ph)
+
+    def tb(g, d):
+        return tbuf.at[d] if g == 0 else dbuf.at[0, d]
+
+    def rb(g, d):
+        return rbuf.at[d] if g == 0 else dbuf.at[0, 2 + d]
 
     def rs(kind, g, c):
         ss, rr = rs_s.at[kind, g, c], rs_r.at[kind, g, c]
@@ -130,16 +133,16 @@
         if kind == D2D:
             return rdma(part.at[g, 1 - core, :, all_of(c)], dbuf.at[g, :, all_of(c)], ss, rr, mate)
         if kind == TUP:
-            return rdma(mine.at[cop, lo_of(c)], tbuf.at[0, g, pl.ds(c * ph, ph)], ss, rr, up)
+            return rdma(mine.at[cop, lo_of(c)], tb(g, 0).at[pl.ds(c * ph, ph)], ss, rr, up)
         if kind == TDN:
-            return rdma(mine.at[cop, hi_of(c)], tbuf.at[1, g, pl.ds(c * ph, ph)], ss, rr, dn)
+            return rdma(mine.at[cop, hi_of(c)], tb(g, 1).at[pl.ds(c * ph, ph)], ss, rr, dn)
         if kind == RUP:
-            return rdma(mine.at[cup, hi_of(c)], rbuf.at[0, g, hi_of(c)], ss, rr, up)
+            return rdma(mine.at[cup, hi_of(c)], rb(g, 0).at[hi_of(c)], ss, rr, up)
         if kind == RDN:
-            return rdma(mine.at[cdn, lo_of(c)], rbuf.at[1, g, lo_of(c)], ss, rr, dn)
+            return rdma(mine.at[cdn, lo_of(c)], rb(g, 1).at[lo_of(c)], ss, rr, dn)
         if kind == SUP:
-            return rdma(mine.at[cup, lo_of(c)], rbuf.at[0, g, lo_of(c)], ss, rr, up)
-        return rdma(mine.at[cdn, hi_of(c)], rbuf.at[1, g, hi_of(c)], ss, rr, dn)
+            return rdma(mine.at[cup, lo_of(c)], rb(g, 0).at[lo_of(c)], ss, rr, up)
+        return rdma(mine.at[cdn, hi_of(c)], rb(g, 1).at[hi_of(c)], ss, rr, dn)
 
     def stage1(g, c):
         rs(D2D, g, c).wait_recv()
@@ -160,7 +163,7 @@
 
             def body(i, _):
                 q = c * pc + off + i
-                a = part[g, core, dst, q].astype(F32) + tbuf[d, g, c * ph + i].astype(F32)
+                a = part[g, core, dst, q].astype(F32) + tb(g, d)[c * ph + i].astype(F32)
                 part[g, core, dst, q] = a.astype(BF16)
                 return 0
 
@@ -176,10 +179,10 @@
         def one(i):
             q = c * pc + i
             z = jnp.sum(jnp.where(lane == g * npair + q, zg, 0.0), axis=1, keepdims=True)
-            a = part[g, core, chip, q].astype(F32) + rbuf[0, g, q].astype(F32) + rbuf[1, g, q].astype(F32)
+            a = part[g, core, chip, q].astype(F32) + rb(g, 0)[q].astype(F32) + rb(g, 1)[q].astype(F32)
             a = a / z
             for j in range(ntile):
-                sbuf[j, pl.ds(pl.multiple_of(q * 16, 16), 16), :] = a[:, j * LANES:(j + 1) * LANES]
+                y2c[j, pl.ds(pl.multiple_of(q * 16, 16), 16), :] = a[:, j * LANES:(j + 1) * LANES]
 
         side_by_side(pc, one)
 
@@ -215,7 +218,7 @@
         def body(q, _):
             for j in range(ntile):
                 part[g, core, chip, q, :, j * LANES:(j + 1) * LANES] = (
-                    sbuf[j, pl.ds(pl.multiple_of(q * 16, 16), 16), :].astype(BF16))
+                    y2c[j, pl.ds(pl.multiple_of(q * 16, 16), 16), :].astype(BF16))
             return 0
 
         lax.fori_loop(0, npair, body, 0)
@@ -235,10 +238,10 @@
         ag(FDN, g, c).wait_recv()
         ag(PHI, g, c).start()
 
-    def logit_at(c, p):
-        each = DTOK // rows
-        return (p // each, pl.ds(pl.multiple_of(p % each * rows, rows), rows),
-                pl.ds(pl.multiple_of(c % (NCHUNK - 1) * cols, cols), cols))
+    nblk = cols // LANES
+
+    def logit_at(c, p, j):
+        return c % (NCHUNK - 1) * nblk + j, pl.ds(pl.multiple_of(p * rows, rows), rows)
 
     def front(c):
         x_load(c).wait()
@@ -270,8 +273,9 @@
             mixb[pl.ds(pl.multiple_of(q * rows, rows), rows), :] = (
                 ex * (1.0 / jnp.sum(ex, axis=1, keepdims=True))).astype(BF16)
             lm = jnp.where(valid, own, NEG_BIG)
-            t, tr, tc = logit_at(c, p)
-            y2c[t, tr, tc] = lm
+            for j in range(nblk):
+                b, sl = logit_at(c, p, j)
+                y2c[b, sl, :] = lm[:, j * LANES:(j + 1) * LANES]
             pm[pl.ds(q, 1), :] = jnp.max(lm, axis=0, keepdims=True)
 
         side_by_side(pc, one)
@@ -294,8 +298,11 @@
 
         def one(p):
             q = c * pc + p
-            t, tr, tc = logit_at(c, p)
-            e = jnp.exp(y2c[t, tr, tc] - mx[pl.ds(q, 1), :])
+            lm = []
+            for j in range(nblk):
+                b, sl = logit_at(c, p, j)
+                lm.append(y2c[b, sl, :])
+            e = jnp.exp(jnp.concatenate(lm, axis=1) - mx[pl.ds(q, 1), :])
             z = jnp.sum(e, axis=0, keepdims=True)
             zs[pl.ds(q, 1), :] = z[:, :half]
             zs[pl.ds(npair + q, 1), :] = z[:, half:]
@@ -320,12 +327,13 @@
             o = dot(h, wso[f:f + step, :])
             acc = o if acc is None else acc + o
 
-        @pl.when(i >= 2)
+        @pl.when(i >= 1)
         def _():
-            y2_store(i - 2, slot).wait()
-
-        y2b[slot] = acc
-        y2_store(i, slot).start()
+            y2_store(i - 1).wait()
+
+        for j in range(ntile):
+            y2b[j] = acc[:, j * LANES:(j + 1) * LANES]
+        y2_store(i).start()
 
         @pl.when(i + 2 < dtiles)
         def _():
@@ -334,7 +342,7 @@
     def expert(g, e, total):
         idx = g * ER + e
         slot = idx % 2
-        xin = jnp.concatenate([sbuf[j, pl.ds(e, 2 * npair, stride=ER), :] for j in range(ntile)], axis=1).astype(BF16)
+        xin = jnp.concatenate([y2c[j, pl.ds(e, 2 * npair, stride=ER), :] for j in range(ntile)], axis=1).astype(BF16)
         l1, l2 = w_load(idx, slot)
         l1.wait()
         l2.wait()
@@ -346,7 +354,7 @@
             o = dot(h, w2b[slot, f:f + step, :])
             acc = o if acc is None else acc + o
         for j in range(ntile):
-            sbuf[j, pl.ds(e, 2 * npair, stride=ER), :] = acc[:, j * LANES:(j + 1) * LANES]
+            y2c[j, pl.ds(e, 2 * npair, stride=ER), :] = acc[:, j * LANES:(j + 1) * LANES]
 
         @pl.when(idx + 2 < total)
         def _():
@@ -362,16 +370,13 @@
                 ag(kind, g, c).wait_recv()
         for t in range(tiles):
             y2_load(c * tiles + t, t).wait()
-            if c > 0:
-                y_store((c - 1) * tiles + t, t).wait()
         for p in range(pc):
             q = c * pc + p
-            t, off = p * rows // DTOK, p * rows % DTOK
             rhs = part[:, :, :, q].reshape(cols, dwidth)
-            yt[t, off:off + rows, :] = (dot(mixb[q * rows:(q + 1) * rows, :], rhs)
-                                        + y2c[t, off:off + rows, :]).astype(BF16)
-        for t in range(tiles):
-            y_store(c * tiles + t, t).start()
+            o = dot(mixb[q * rows:(q + 1) * rows, :], rhs)
+            for j in range(ntile):
+                y_ref[q * rows:(q + 1) * rows, j * LANES:(j + 1) * LANES] = (
+                    o[:, j * LANES:(j + 1) * LANES] + y2c[j, p * rows:(p + 1) * rows, :]).astype(BF16)
 
     for c in range(NCHUNK):
         x_load(c).start()
@@ -480,16 +485,13 @@
            (1, relay1, 1, 0), (1, send_own, 1, 2),
            (3, relay1, 1, 1), (3, send_own, 1, 3), (4, relay2, 1, 0), (5, relay1, 1, 2), (5, combine, 0, 0),
            (5, prefetch, 0, 1), (6, relay2, 1, 1), (6, combine, 0, 1), (6, prefetch, 0, 2), (6, relay1, 1, 3)))
-    for i in (dtiles - 2, dtiles - 1):
-        y2_store(i, i % 2).wait()
+    y2_store(dtiles - 1).wait()
     relay2(1, 2)
     combine(0, 2)
     prefetch(0, 3)
     relay2(1, 3)
     combine(0, 3)
 
-    for t in range(tiles):
-        y_store(dtiles - tiles + t, t).wait()
     for k in range(1, n):
         z_msg(k).wait_send()
 
@@ -531,25 +533,23 @@
             in_specs=[pl.BlockSpec(memory_space=pltpu.SMEM), pl.BlockSpec(memory_space=pltpu.SMEM),
                       pl.BlockSpec(memory_space=pltpu.VMEM), pl.BlockSpec(memory_space=pltpu.VMEM),
                       any_spec, any_spec, any_spec, any_spec, any_spec],
-            out_specs=[any_spec, any_spec, any_spec],
-            out_shape=[jax.ShapeDtypeStruct((ntok, width), BF16),
-                       jax.ShapeDtypeStruct((ntok, width), F32),
+            out_specs=[pl.BlockSpec(memory_space=pltpu.VMEM), any_spec, any_spec],
+            out_shape=[pltpu.VMEM((ntok, width), BF16),
+                       jax.ShapeDtypeStruct((width // LANES, ntok, LANES), F32),
                        jax.ShapeDtypeStruct((ntok, width), BF16)],
             scratch_shapes=[
                 pltpu.VMEM((NGRP, 2, chips, npair, 16, width), BF16),
                 pltpu.VMEM((NGRP, chips, npair, 16, width), BF16),
-                pltpu.VMEM((2, NGRP, npair // 2, 16, width), BF16),
-                pltpu.VMEM((2, NGRP, npair, 16, width), BF16),
+                pltpu.VMEM((2, npair // 2, 16, width), BF16),
+                pltpu.VMEM((2, npair, 16, width), BF16),
                 pltpu.VMEM((width, hidden), BF16),
                 pltpu.VMEM((hidden, width), BF16),
                 pltpu.VMEM((2, width, hidden), BF16),
                 pltpu.VMEM((2, hidden, width), BF16),
                 pltpu.VMEM((ntok, cols), BF16),
                 pltpu.VMEM((2, DTOK, width), BF16),
-                pltpu.VMEM((2, DTOK, width), F32),
-                pltpu.VMEM((pc * rows // DTOK, DTOK, width), F32),
-                pltpu.VMEM((pc * rows // DTOK, DTOK, width), BF16),
-                pltpu.VMEM((width // LANES, npair * 16, LANES), F32),
+                pltpu.VMEM((width // LANES, DTOK, LANES), F32),
+                pltpu.VMEM((width // LANES, pc * rows, LANES), F32),
                 pltpu.VMEM((width, cols), BF16),
                 pltpu.VMEM((npair, cols), F32),
                 pltpu.VMEM((n, npair, cols), F32),
@@ -561,11 +561,11 @@
                 sem((7, NGRP, NCHUNK)), sem((7, NGRP, NCHUNK)),
                 sem((9, NGRP, NCHUNK)), sem((9, NGRP, NCHUNK)),
                 sem((n - 1, NCHUNK)), sem((n - 1, NCHUNK)), sem((n - 1,)), sem((n - 1,)),
-                sem((NCHUNK,)), sem((2,)), sem((2,)), sem((2, 2)), sem((2,)), sem((2,)),
-                sem((pc * rows // DTOK,)), sem((pc * rows // DTOK,)), pltpu.SemaphoreType.REGULAR((NGRP,)),
+                sem((NCHUNK,)), sem((2,)), sem((2,)), sem((2, 2)), sem((2,)), sem(()),
+                sem((pc * rows // DTOK,)), pltpu.SemaphoreType.REGULAR((NGRP,)),
             ],
             compiler_params=pltpu.CompilerParams(collective_id=0, has_side_effects=True,
-                                                 vmem_limit_bytes=VMEM_BYTES),
+                                                 vmem_limit_bytes=VMEM_BYTES - ntok * width * 2),
             name='mega',
         )(len_blk, scale_g.reshape(1), phi_slots, perm, x2, ws_in, ws_out, w_in_blk, w_out_blk)
         return y.reshape(batch, tok, width)

time: 138 us -> 133 us (0.964)
  local copies, waits for them, and re-layouts: 6.24 us -> 2.71 us
    unnamed x1, local copies, waits for them, and re-layouts: 6.24 us -> 2.71 us
    pallas_call x1, Pallas kernels: 131 us -> 130 us  [per_device(): pl.pallas_call(functools.partial(mega_kernel, n, tok), in_specs=[pl.Block...]
where the time goes in v3:
time: 133 us
  Pallas kernels  130 us (98%)
  local copies, waits for them, and re-layouts  2.71 us (2%)
    pallas_call x1, Pallas kernels, per_device(): pl.pallas_call(functools.partial(mega_kernel, n, tok), in_specs=[pl.Block...  130 us
    unnamed x1, local copies, waits for them, and re-layouts  2.71 us

profile of v3, /device:TPU:113, one launch (start us, length us, event | category | flops | bytes accessed | tf_op | source)
XLA Modules:
  0.0 133.2 jit_solution(17730668400541684921)
XLA Ops:
  0.7 129.9 %mega.1 = (bf16[4096,768]{1,0:T(8,128)(2,1)S(1)}, f32[6,4096,128]{2,1,0:T(8,128)}, bf16[4096,768]{1,0:T(8,128)(2,1)}) custom-call(s32[64]{0:T(128)} %len_ref.1, f32[1]{0:T(128)} %bitcast.3.gain_ref, bf16[768,128]{1,0:T(8,128)(2,1)} %phi_ref.1, bf16[128,256]{1,0:T(8,128)(2,1)} %constant.2.clone.perm_ref, bf16[4096,768]{1,0:T(8,128)(2,1)} %bitcast.5, ...), custom_call_target="tpu_custom_call" | custom-call | tf_op jit(solution)/shard_map/mega/pallas_call | solution.py:531
  130.5 2.7 %copy.11 = bf16[64,64,768]{2,1,0:T(8,128)(2,1)} copy(bf16[64,64,768]{2,1,0:T(8,128)(2,1)S(1)} %bitcast.4) | data formatting | bytes 12582912

commit v4 on v3

--- a/solution.py
+++ b/solution.py
@@ -346,13 +346,7 @@
         l1, l2 = w_load(idx, slot)
         l1.wait()
         l2.wait()
-        hidden = w1b.shape[2]
-        step = min(hidden, 768)
-        acc = None
-        for f in range(0, hidden, step):
-            h = gelu(dot(xin, w1b[slot, :, f:f + step])).astype(BF16)
-            o = dot(h, w2b[slot, f:f + step, :])
-            acc = o if acc is None else acc + o
+        acc = dot(gelu(dot(xin, w1b[slot])).astype(BF16), w2b[slot])
         for j in range(ntile):
             y2c[j, pl.ds(e, 2 * npair, stride=ER), :] = acc[:, j * LANES:(j + 1) * LANES]
 

time: 133 us -> 131 us (0.985)
  Pallas kernels: 130 us -> 128 us
    pallas_call x1, Pallas kernels: 130 us -> 128 us  [per_device(): pl.pallas_call(functools.partial(mega_kernel, n, tok), in_specs=[pl.Block...]
where the time goes in v4:
time: 131 us
  Pallas kernels  128 us (98%)
  local copies, waits for them, and re-layouts  2.71 us (2%)
    pallas_call x1, Pallas kernels, per_device(): pl.pallas_call(functools.partial(mega_kernel, n, tok), in_specs=[pl.Block...  128 us
    unnamed x1, local copies, waits for them, and re-layouts  2.71 us

profile of v4, /device:TPU:113, one launch (start us, length us, event | category | flops | bytes accessed | tf_op | source)
XLA Modules:
  0.0 131.1 jit_solution(15792443142408245707)
XLA Ops:
  0.7 127.7 %mega.1 = (bf16[4096,768]{1,0:T(8,128)(2,1)S(1)}, f32[6,4096,128]{2,1,0:T(8,128)}, bf16[4096,768]{1,0:T(8,128)(2,1)}) custom-call(s32[64]{0:T(128)} %len_ref.1, f32[1]{0:T(128)} %bitcast.3.gain_ref, bf16[768,128]{1,0:T(8,128)(2,1)} %phi_ref.1, bf16[128,256]{1,0:T(8,128)(2,1)} %constant.2.clone.perm_ref, bf16[4096,768]{1,0:T(8,128)(2,1)} %bitcast.5, ...), custom_call_target="tpu_custom_call" | custom-call | tf_op jit(solution)/shard_map/mega/pallas_call | solution.py:525
  128.3 2.7 %copy.11 = bf16[64,64,768]{2,1,0:T(8,128)(2,1)} copy(bf16[64,64,768]{2,1,0:T(8,128)(2,1)S(1)} %bitcast.4) | data formatting | bytes 12582912
